TPU v7x, 32 devices: a whole 2x2x4 slice. The times are simulated.
32 devices in a mesh: section: 4 (over y, x), fsdp: 8 (over z, core).
Axes of the slice: x: 2, y: 2, z: 4, core: 2. Of those that a mesh axis runs over, the one named last changes fastest.
Arguments:
- grad_parts: bfloat16 [4, 8, 8192, 1024], P('section', 'fsdp'), may hold values from -510 to 510
- first_codes: int32 [4, 8192, 1024], P('section', 'fsdp'), may hold values from -7 to 7
- first_rows: float32 [4, 8192], P('section', 'fsdp'), may hold values from 0.003 to 0.03
- first_columns: float32 [4, 1024], P('section'), may hold values from 0.003 to 0.03
- second_codes: int32 [4, 8192, 1024], P('section', 'fsdp'), may hold values from 1 to 15
- second_rows: float32 [4, 8192], P('section', 'fsdp'), may hold values from 0.001 to 0.01
- second_columns: float32 [4, 1024], P('section'), may hold values from 0.001 to 0.01
Outputs:
- direction: float32 [4, 8192, 1024], P('section', 'fsdp')
- first_scaled: float32 [4, 8192, 1024], P('section', 'fsdp')
- second_scaled: float32 [4, 8192, 1024], P('section', 'fsdp')
- first_rowmax: float32 [4, 8192], P('section', 'fsdp')
- first_colmax: float32 [4, 1024], P('section')
- second_rowmax: float32 [4, 8192], P('section', 'fsdp')
- second_colmax: float32 [4, 1024], P('section')
All inputs are finite; a program needn't handle non-finite values. Where the computation divides by a largest or mean magnitude, that divisor is 1e-20 or more.
Results may differ from a plain program's by a relative error of at most 0.0003.
Values may be sent and summed in bfloat16 or wider, within the bound.
A program may use at most 192 MiB of HBM per device.

v0:
```python
import functools
import math

import jax
import jax.numpy as jnp
from jax import lax
from jax.experimental import pallas as pl
from jax.experimental.pallas import tpu as pltpu
from jax.sharding import PartitionSpec as P

beta_first = 0.9
beta_second = 0.999
clip_rms = 3.0
epsilon = 1e-08
scale_floor = 0.001

CORES = 2
SLAB = 128
LANES = 128
LAG = 2
VMEM_BYTES = 67043328
F32 = jnp.float32


def exchange_kernel(
    chips,
    fsdp,
    sections,
    slabs,
    clip_limit,
    grads,
    first_codes,
    first_rows,
    first_cols,
    second_codes,
    second_rows,
    second_cols,
    first_out,
    second_out,
    first_colmax,
    second_colmax,
    own,
    part,
    right_sum,
    left_sum,
    total,
    codes_a,
    codes_b,
    first,
    second,
    square_send,
    square_recv,
    cross_send,
    cross_recv,
    col_send,
    col_recv,
    own_sem,
    part_send_sem,
    part_recv_sem,
    right_send_sem,
    right_recv_sem,
    left_send_sem,
    left_recv_sem,
    code_sem,
    out_sem,
    square_sems,
    cross_sems,
    col_sems,
):
    me = lax.axis_index("fsdp")
    section = lax.axis_index("section")
    chip = me // CORES
    core = me % CORES
    partner = chip * CORES + (1 - core)
    right = ((chip + 1) % chips) * CORES + core
    left = ((chip + chips - 1) % chips) * CORES + core
    cols = total.shape[-1]
    items = (chips - 1) * slabs

    def own_copy(dest, slab):
        return pltpu.make_async_copy(
            grads.at[dest, core, slab], own.at[dest, slab], own_sem.at[dest * slabs + slab]
        )

    def part_copy(dest, slab):
        return pltpu.make_async_remote_copy(
            src_ref=grads.at[dest, 1 - core, slab],
            dst_ref=part.at[dest, slab],
            send_sem=part_send_sem.at[dest * slabs + slab],
            recv_sem=part_recv_sem.at[dest * slabs + slab],
            device_id={"fsdp": partner},
            device_id_type=pl.DeviceIdType.MESH,
        )

    def right_copy(dest, slab):
        slot = (dest - 1) * slabs + slab
        return pltpu.make_async_remote_copy(
            src_ref=right_sum.at[dest - 1, slab],
            dst_ref=right_sum.at[dest - 1, slab],
            send_sem=right_send_sem.at[slot],
            recv_sem=right_recv_sem.at[slot],
            device_id={"fsdp": right},
            device_id_type=pl.DeviceIdType.MESH,
        )

    def left_copy(dest, slab):
        slot = dest * slabs + slab
        return pltpu.make_async_remote_copy(
            src_ref=left_sum.at[dest, slab],
            dst_ref=left_sum.at[dest, slab],
            send_sem=left_send_sem.at[slot],
            recv_sem=left_recv_sem.at[slot],
            device_id={"fsdp": left},
            device_id_type=pl.DeviceIdType.MESH,
        )

    def wait_pair(dest, slab):
        own_copy(dest, slab).wait()
        part_copy(dest, slab).wait_recv()

    def pair_sum(dest, slab):
        return own[dest, slab].astype(F32) + part[dest, slab].astype(F32)

    @pl.loop(0, chips * slabs)
    def _(i):
        step, slab = i // slabs, i % slabs
        dest = jnp.where(2 * chip < chips, chips - 1 - step, step)
        own_copy(dest, slab).start()
        part_copy(dest, slab).start()

    code_copies = (
        pltpu.make_async_copy(first_codes, codes_a, code_sem.at[0]),
        pltpu.make_async_copy(second_codes, codes_b, code_sem.at[1]),
    )
    for copy in code_copies:
        copy.start()

    @pl.when(chip == 0)
    def _():
        @pl.loop(0, items)
        def _(j):
            dest, slab = chips - 1 - j // slabs, j % slabs
            wait_pair(dest, slab)
            right_sum[dest - 1, slab] = pair_sum(dest, slab)
            right_copy(dest, slab).start()

    @pl.when(chip == chips - 1)
    def _():
        @pl.loop(0, items)
        def _(j):
            dest, slab = j // slabs, j % slabs
            wait_pair(dest, slab)
            left_sum[dest, slab] = pair_sum(dest, slab)
            left_copy(dest, slab).start()

    @pl.loop(0, slabs)
    def _(slab):
        wait_pair(chip, slab)
        total[slab] = pair_sum(chip, slab)

    for copy in code_copies:
        copy.wait()

    @pl.loop(0, slabs)
    def _(slab):
        rows = pl.ds(pl.multiple_of(slab * SLAB, SLAB), SLAB)
        first_row = jnp.broadcast_to(first_rows[:, rows], (LANES, SLAB)).T
        second_row = jnp.broadcast_to(second_rows[:, rows], (LANES, SLAB)).T
        for q in range(cols // LANES):
            span = pl.ds(q * LANES, LANES)
            first_bound = jnp.minimum(first_row, first_cols[:, span])
            second_bound = jnp.minimum(second_row, second_cols[:, span])
            first_old = codes_a[slab, :, span].astype(F32) / 7.0 * first_bound
            second_old = codes_b[slab, :, span].astype(F32) / 15.0 * second_bound
            first[slab, :, span] = beta_first * first_old
            second[slab, :, span] = beta_second * second_old

    right_lag = LAG * chip
    left_lag = LAG * (chips - 1 - chip)

    @pl.loop(0, items + LAG * (chips - 1))
    def _(step):
        j = step - right_lag
        dest = chips - 1 - j // slabs
        slab = j % slabs

        @pl.when((chip > 0) & (j >= 0) & (dest > chip))
        def _():
            right_copy(dest, slab).wait_recv()
            wait_pair(dest, slab)
            right_sum[dest - 1, slab] += pair_sum(dest, slab)
            right_copy(dest, slab).start()

        @pl.when((chip > 0) & (j >= 0) & (dest == chip))
        def _():
            right_copy(dest, slab).wait_recv()
            total[slab] += right_sum[dest - 1, slab]

        i = step - left_lag
        low = i // slabs
        strip = i % slabs

        @pl.when((chip < chips - 1) & (i >= 0) & (low < chip))
        def _():
            left_copy(low, strip).wait_recv()
            wait_pair(low, strip)
            left_sum[low, strip] += pair_sum(low, strip)
            left_copy(low, strip).start()

        @pl.when((chip < chips - 1) & (i >= 0) & (low == chip))
        def _():
            left_copy(low, strip).wait_recv()
            total[strip] += left_sum[low, strip]

    piece = 16
    pieces = SLAB // piece

    def add_squares(i, acc):
        slab, rows = i // pieces, pl.ds(pl.multiple_of((i % pieces) * piece, piece), piece)
        g = total[slab, rows, :]
        return acc + jnp.sum((g * g).reshape(piece // 8, 8, cols), axis=0)

    squares = lax.fori_loop(0, slabs * pieces, add_squares, jnp.zeros((8, cols), F32))
    folded = squares[:, :LANES]
    for q in range(1, cols // LANES):
        folded = folded + squares[:, q * LANES : (q + 1) * LANES]

    def to_all(axis, size, position, source, slots, sems):
        copies = [
            pltpu.make_async_remote_copy(
                src_ref=source,
                dst_ref=slots.at[s - 1],
                send_sem=sems.at[0, s - 1],
                recv_sem=sems.at[1, s - 1],
                device_id={axis: (position + s) % size},
                device_id_type=pl.DeviceIdType.MESH,
            )
            for s in range(1, size)
        ]
        for copy in copies:
            copy.start()
        return copies

    square_send[...] = folded
    square_copies = to_all("fsdp", fsdp, me, square_send, square_recv, square_sems)
    for s, copy in enumerate(square_copies):
        copy.wait_recv()
        folded = folded + square_recv[s]
    cross_send[...] = folded
    cross_copies = to_all("section", sections, section, cross_send, cross_recv, cross_sems)
    for s, copy in enumerate(cross_copies):
        copy.wait_recv()
        folded = folded + cross_recv[s]
    square_sum = jnp.sum(jnp.sum(folded, axis=0, keepdims=True), axis=1, keepdims=True)
    norm = jnp.sqrt(jnp.broadcast_to(square_sum, (1, cols)))
    scale = clip_limit / jnp.maximum(norm, clip_limit)

    def out_copies(slab):
        return (
            pltpu.make_async_copy(first.at[slab], first_out.at[slab], out_sem.at[0, slab]),
            pltpu.make_async_copy(second.at[slab], second_out.at[slab], out_sem.at[1, slab]),
        )

    def update_slab(slab, carry):
        def update_piece(i, carry):
            first_top, second_top = carry
            rows = pl.ds(pl.multiple_of(i * piece, piece), piece)
            clipped = scale * total[slab, rows, :]
            first_new = first[slab, rows, :] + (1.0 - beta_first) * clipped
            second_new = second[slab, rows, :] + (1.0 - beta_second) * clipped * clipped
            first[slab, rows, :] = first_new
            second[slab, rows, :] = second_new
            high = jnp.max(jnp.abs(first_new).reshape(piece // 8, 8, cols), axis=0)
            top = jnp.max(second_new.reshape(piece // 8, 8, cols), axis=0)
            return jnp.maximum(first_top, high), jnp.maximum(second_top, top)

        carry = lax.fori_loop(0, pieces, update_piece, carry)
        for copy in out_copies(slab):
            copy.start()
        return carry

    nothing = jnp.zeros((8, cols), F32)
    first_top, second_top = lax.fori_loop(0, slabs, update_slab, (nothing, nothing))
    first_top = jnp.max(first_top, axis=0, keepdims=True)
    second_top = jnp.max(second_top, axis=0, keepdims=True)
    col_send[0:1, :] = first_top
    col_send[1:2, :] = second_top
    col_copies = to_all("fsdp", fsdp, me, col_send, col_recv, col_sems)

    @pl.loop(0, chips * slabs)
    def _(i):
        part_copy(i // slabs, i % slabs).wait_send()

    @pl.loop(0, items)
    def _(j):
        slab = j % slabs

        @pl.when(j // slabs + 1 > chip)
        def _():
            right_copy(j // slabs + 1, slab).wait_send()

        @pl.when(j // slabs < chip)
        def _():
            left_copy(j // slabs, slab).wait_send()

    for copy in square_copies + cross_copies:
        copy.wait_send()

    for s, copy in enumerate(col_copies):
        copy.wait_recv()
        first_top = jnp.maximum(first_top, col_recv[s, 0:1, :])
        second_top = jnp.maximum(second_top, col_recv[s, 1:2, :])
    first_colmax[...] = jnp.maximum(first_top, scale_floor)
    second_colmax[...] = second_top
    for copy in col_copies:
        copy.wait_send()

    @pl.loop(0, slabs)
    def _(slab):
        for copy in out_copies(slab):
            copy.wait()


def finish_kernel(
    first,
    second,
    first_colmax,
    second_colmax,
    direction,
    first_scaled,
    second_scaled,
    first_rowmax,
    second_rowmax,
    first_kept,
    second_kept,
):
    first_new = first[0]
    second_new = second[0]
    first_top = jnp.maximum(jnp.max(jnp.abs(first_new), axis=1, keepdims=True), scale_floor)
    second_top = jnp.max(second_new, axis=1, keepdims=True)
    direction[0] = first_new / (jnp.sqrt(second_new) + epsilon)
    first_scaled[0] = first_new / jnp.minimum(first_top, first_colmax[...])
    second_scaled[0] = second_new / jnp.minimum(second_top, second_colmax[...])
    first_rowmax[...] = jnp.broadcast_to(first_top, (SLAB, LANES)).T[0:1, :]
    second_rowmax[...] = jnp.broadcast_to(second_top, (SLAB, LANES)).T[0:1, :]
    first_kept[...] = first_colmax[...]
    second_kept[...] = second_colmax[...]


def local(
    grad_parts, first_codes, first_rows, first_columns, second_codes, second_rows, second_columns
):
    fsdp = lax.axis_size("fsdp")
    sections = lax.axis_size("section")
    layers, _, row_count, cols = grad_parts.shape
    chips = fsdp // CORES
    rows = row_count // fsdp
    slabs = rows // SLAB
    clip_limit = clip_rms * math.sqrt(layers * sections * row_count * cols)
    grads = grad_parts.reshape(chips, CORES, slabs, SLAB, cols)
    tiled = (slabs, SLAB, cols)
    items = (chips - 1) * slabs
    hbm = pl.BlockSpec(memory_space=pl.ANY)
    vmem = pl.BlockSpec(memory_space=pltpu.VMEM)
    dma = pltpu.SemaphoreType.DMA
    first_new, second_new, first_colmax, second_colmax = pl.pallas_call(
        functools.partial(exchange_kernel, chips, fsdp, sections, slabs, clip_limit),
        out_shape=(
            jax.ShapeDtypeStruct(tiled, F32),
            jax.ShapeDtypeStruct(tiled, F32),
            jax.ShapeDtypeStruct((1, cols), F32),
            jax.ShapeDtypeStruct((1, cols), F32),
        ),
        in_specs=[hbm, hbm, vmem, vmem, hbm, vmem, vmem],
        out_specs=(hbm, hbm, vmem, vmem),
        scratch_shapes=[
            pltpu.VMEM((chips, *tiled), jnp.bfloat16),
            pltpu.VMEM((chips, *tiled), jnp.bfloat16),
            pltpu.VMEM((chips - 1, *tiled), F32),
            pltpu.VMEM((chips - 1, *tiled), F32),
            pltpu.VMEM(tiled, F32),
            pltpu.VMEM(tiled, jnp.int32),
            pltpu.VMEM(tiled, jnp.int32),
            pltpu.VMEM(tiled, F32),
            pltpu.VMEM(tiled, F32),
            pltpu.VMEM((8, LANES), F32),
            pltpu.VMEM((fsdp - 1, 8, LANES), F32),
            pltpu.VMEM((8, LANES), F32),
            pltpu.VMEM((max(sections - 1, 1), 8, LANES), F32),
            pltpu.VMEM((2, cols), F32),
            pltpu.VMEM((fsdp - 1, 2, cols), F32),
            dma((chips * slabs,)),
            dma((chips * slabs,)),
            dma((chips * slabs,)),
            dma((items,)),
            dma((items,)),
            dma((items,)),
            dma((items,)),
            dma((2,)),
            dma((2, slabs)),
            dma((2, fsdp - 1)),
            dma((2, max(sections - 1, 1))),
            dma((2, fsdp - 1)),
        ],
        compiler_params=pltpu.CompilerParams(
            has_side_effects=True, vmem_limit_bytes=VMEM_BYTES
        ),
    )(
        grads,
        first_codes.reshape(tiled),
        first_rows,
        first_columns,
        second_codes.reshape(tiled),
        second_rows,
        second_columns,
    )
    block = pl.BlockSpec((1, SLAB, cols), lambda i: (i, 0, 0))
    whole = pl.BlockSpec((1, cols), lambda i: (0, 0))
    strip = pl.BlockSpec((1, SLAB), lambda i: (0, i))
    finished = pl.pallas_call(
        finish_kernel,
        grid=(slabs,),
        out_shape=(
            jax.ShapeDtypeStruct(tiled, F32),
            jax.ShapeDtypeStruct(tiled, F32),
            jax.ShapeDtypeStruct(tiled, F32),
            jax.ShapeDtypeStruct((1, rows), F32),
            jax.ShapeDtypeStruct((1, rows), F32),
            jax.ShapeDtypeStruct((1, cols), F32),
            jax.ShapeDtypeStruct((1, cols), F32),
        ),
        in_specs=[block, block, whole, whole],
        out_specs=(block, block, block, strip, strip, whole, whole),
    )(first_new, second_new, first_colmax, second_colmax)
    direction, first_scaled, second_scaled = finished[:3]
    first_rowmax, second_rowmax, first_colmax, second_colmax = finished[3:]
    shape = (layers, rows, cols)
    return (
        direction.reshape(shape),
        first_scaled.reshape(shape),
        second_scaled.reshape(shape),
        first_rowmax,
        first_colmax,
        second_rowmax,
        second_colmax,
    )


def solution(mesh):
    placed = (
        P("section", "fsdp", None, None),
        P("section", "fsdp", None),
        P("section", "fsdp"),
        P("section", None),
        P("section", "fsdp", None),
        P("section", "fsdp"),
        P("section", None),
    )
    return jax.shard_map(
        local,
        mesh=mesh,
        in_specs=placed,
        out_specs=(
            P("section", "fsdp", None),
            P("section", "fsdp", None),
            P("section", "fsdp", None),
            P("section", "fsdp"),
            P("section", None),
            P("section", "fsdp"),
            P("section", None),
        ),
        check_vma=False,
    )
```

profile of v0, /device:TPU:0, one launch (start us, length us, event | category | flops | bytes accessed | tf_op | source)
XLA Modules:
  0.0 310.5 jit_solution(17252369706925334506)
XLA Ops:
  0.6 299.4 %shard_map.126 = (f32[8,128,1024]{2,1,0:T(8,128)}, f32[8,128,1024]{2,1,0:T(8,128)}, f32[1,1024]{1,0:T(1,128)}, f32[1,1024]{1,0:T(1,128)}) custom-call(bf16[4,2,8,128,1024]{4,3,2,1,0:T(8,128)(2,1)} %bitcast.6, s32[8,128,1024]{2,1,0:T(8,128)} %bitcast.7, f32[1,1024]{1,0:T(1,128)} %first_rows.1, f32[1,1024]{1,0:T(1,128)} %first_cols.1, ...), custom_call_target="tpu_custom_call" | custom-call | tf_op jit(solution)/shard_map/pallas_call | solution.py:366
  300.0 10.4 %shard_map.127 = (f32[8,128,1024]{2,1,0:T(8,128)}, f32[8,128,1024]{2,1,0:T(8,128)}, f32[8,128,1024]{2,1,0:T(8,128)}, f32[1,1024]{1,0:T(1,128)}, f32[1,1024]{1,0:...) custom-call(f32[8,128,1024]{2,1,0:T(8,128)} %get-tuple-element.18.first, f32[8,128,1024]{2,1,0:T(8,128)} %get-tuple-element.19.second, ...), custom_call_target="tpu_custom_call" | custom-call | tf_op jit(solution)/shard_map/pallas_call | solution.py:420
where the time goes:
time: 311 us; the launch traced here: 310 us
  Pallas kernels  310 us (100%)
    pallas_call x1, Pallas kernels, local(): pl.pallas_call(functools.partial(exchange_kernel, chips, fsdp, sections,...  299 us
    pallas_call x1, Pallas kernels, local(): pl.pallas_call(finish_kernel, grid=(slabs,), out_shape=(jax.ShapeDtypeStr...  10.4 us

commit v1 on v0

--- a/solution.py
+++ b/solution.py
@@ -18,6 +18,9 @@
 SLAB = 128
 LANES = 128
 LAG = 2
+PIECE = 16
+LEVELS = 32767.0
+TINY = 1e-37
 VMEM_BYTES = 67043328
 F32 = jnp.float32
 
@@ -41,8 +44,11 @@
     second_colmax,
     own,
     part,
-    right_sum,
-    left_sum,
+    right_code,
+    left_code,
+    right_top,
+    left_top,
+    stage,
     total,
     codes_a,
     codes_b,
@@ -57,10 +63,8 @@
     own_sem,
     part_send_sem,
     part_recv_sem,
-    right_send_sem,
-    right_recv_sem,
-    left_send_sem,
-    left_recv_sem,
+    right_sems,
+    left_sems,
     code_sem,
     out_sem,
     square_sems,
@@ -92,34 +96,90 @@
             device_id_type=pl.DeviceIdType.MESH,
         )
 
-    def right_copy(dest, slab):
-        slot = (dest - 1) * slabs + slab
-        return pltpu.make_async_remote_copy(
-            src_ref=right_sum.at[dest - 1, slab],
-            dst_ref=right_sum.at[dest - 1, slab],
-            send_sem=right_send_sem.at[slot],
-            recv_sem=right_recv_sem.at[slot],
-            device_id={"fsdp": right},
-            device_id_type=pl.DeviceIdType.MESH,
+    def hop(wire, tops, sems, slot, target):
+        return tuple(
+            pltpu.make_async_remote_copy(
+                src_ref=ref.at[slot],
+                dst_ref=ref.at[slot],
+                send_sem=sems.at[2 * kind, slot],
+                recv_sem=sems.at[2 * kind + 1, slot],
+                device_id={"fsdp": target},
+                device_id_type=pl.DeviceIdType.MESH,
+            )
+            for kind, ref in enumerate((wire, tops))
         )
 
-    def left_copy(dest, slab):
-        slot = dest * slabs + slab
-        return pltpu.make_async_remote_copy(
-            src_ref=left_sum.at[dest, slab],
-            dst_ref=left_sum.at[dest, slab],
-            send_sem=left_send_sem.at[slot],
-            recv_sem=left_recv_sem.at[slot],
-            device_id={"fsdp": left},
-            device_id_type=pl.DeviceIdType.MESH,
-        )
+    def right_slot(dest, slab):
+        return (dest - 1) * slabs + slab
+
+    def left_slot(dest, slab):
+        return dest * slabs + slab
+
+    def right_hop(slot):
+        return hop(right_code, right_top, right_sems, slot, right)
+
+    def left_hop(slot):
+        return hop(left_code, left_top, left_sems, slot, left)
+
+    def start(copies):
+        for copy in copies:
+            copy.start()
+
+    def wait_recv(copies):
+        for copy in copies:
+            copy.wait_recv()
+
+    def piece_rows(i):
+        return pl.ds(pl.multiple_of(i * PIECE, PIECE), PIECE)
+
+    def encode(term, wire, tops, slot):
+        def collect(i, high):
+            rows = piece_rows(i)
+            value = term(rows)
+            stage[rows, :] = value
+            return jnp.maximum(
+                high, jnp.max(jnp.abs(value).reshape(PIECE // 8, 8, cols), axis=0)
+            )
+
+        high = lax.fori_loop(0, SLAB // PIECE, collect, jnp.zeros((8, cols), F32))
+        top = jnp.maximum(jnp.max(high, axis=0, keepdims=True), TINY)
+        tops[slot] = top
+        gain = LEVELS * lax.rsqrt(top)
+
+        @pl.loop(0, SLAB // PIECE)
+        def _(i):
+            rows = piece_rows(i)
+            value = stage[rows, :]
+            root = value * lax.rsqrt(jnp.maximum(jnp.abs(value), TINY))
+            wire[slot, rows, :] = jnp.round(root * gain).astype(jnp.int32).astype(jnp.int16)
+
+    def decoder(wire, tops, slot):
+        unit = tops[slot] * (1.0 / (LEVELS * LEVELS))
+
+        def decode(rows):
+            code = wire[slot, rows, :].astype(jnp.int32).astype(F32)
+            return code * jnp.abs(code) * unit
+
+        return decode
+
+    def add_total(slab, decode):
+        @pl.loop(0, SLAB // PIECE)
+        def _(i):
+            rows = piece_rows(i)
+            total[slab, rows, :] += decode(rows)
 
     def wait_pair(dest, slab):
         own_copy(dest, slab).wait()
         part_copy(dest, slab).wait_recv()
 
     def pair_sum(dest, slab):
-        return own[dest, slab].astype(F32) + part[dest, slab].astype(F32)
+        def term(rows):
+            return own[dest, slab, rows, :].astype(F32) + part[dest, slab, rows, :].astype(F32)
+
+        return term
+
+    def joined(decode, pair):
+        return lambda rows: decode(rows) + pair(rows)
 
     @pl.loop(0, chips * slabs)
     def _(i):
@@ -141,8 +201,9 @@
         def _(j):
             dest, slab = chips - 1 - j // slabs, j % slabs
             wait_pair(dest, slab)
-            right_sum[dest - 1, slab] = pair_sum(dest, slab)
-            right_copy(dest, slab).start()
+            slot = right_slot(dest, slab)
+            encode(pair_sum(dest, slab), right_code, right_top, slot)
+            start(right_hop(slot))
 
     @pl.when(chip == chips - 1)
     def _():
@@ -150,13 +211,19 @@
         def _(j):
             dest, slab = j // slabs, j % slabs
             wait_pair(dest, slab)
-            left_sum[dest, slab] = pair_sum(dest, slab)
-            left_copy(dest, slab).start()
+            slot = left_slot(dest, slab)
+            encode(pair_sum(dest, slab), left_code, left_top, slot)
+            start(left_hop(slot))
 
     @pl.loop(0, slabs)
     def _(slab):
         wait_pair(chip, slab)
-        total[slab] = pair_sum(chip, slab)
+        term = pair_sum(chip, slab)
+
+        @pl.loop(0, SLAB // PIECE)
+        def _(i):
+            rows = piece_rows(i)
+            total[slab, rows, :] = term(rows)
 
     for copy in code_copies:
         copy.wait()
@@ -184,33 +251,41 @@
         dest = chips - 1 - j // slabs
         slab = j % slabs
 
-        @pl.when((chip > 0) & (j >= 0) & (dest > chip))
+        @pl.when((chip > 0) & (j >= 0) & (dest >= chip))
         def _():
-            right_copy(dest, slab).wait_recv()
-            wait_pair(dest, slab)
-            right_sum[dest - 1, slab] += pair_sum(dest, slab)
-            right_copy(dest, slab).start()
-
-        @pl.when((chip > 0) & (j >= 0) & (dest == chip))
-        def _():
-            right_copy(dest, slab).wait_recv()
-            total[slab] += right_sum[dest - 1, slab]
+            slot = right_slot(dest, slab)
+            wait_recv(right_hop(slot))
+            decode = decoder(right_code, right_top, slot)
+
+            @pl.when(dest > chip)
+            def _():
+                wait_pair(dest, slab)
+                encode(joined(decode, pair_sum(dest, slab)), right_code, right_top, slot)
+                start(right_hop(slot))
+
+            @pl.when(dest == chip)
+            def _():
+                add_total(slab, decode)
 
         i = step - left_lag
         low = i // slabs
         strip = i % slabs
 
-        @pl.when((chip < chips - 1) & (i >= 0) & (low < chip))
+        @pl.when((chip < chips - 1) & (i >= 0) & (low <= chip))
         def _():
-            left_copy(low, strip).wait_recv()
-            wait_pair(low, strip)
-            left_sum[low, strip] += pair_sum(low, strip)
-            left_copy(low, strip).start()
-
-        @pl.when((chip < chips - 1) & (i >= 0) & (low == chip))
-        def _():
-            left_copy(low, strip).wait_recv()
-            total[strip] += left_sum[low, strip]
+            slot = left_slot(low, strip)
+            wait_recv(left_hop(slot))
+            decode = decoder(left_code, left_top, slot)
+
+            @pl.when(low < chip)
+            def _():
+                wait_pair(low, strip)
+                encode(joined(decode, pair_sum(low, strip)), left_code, left_top, slot)
+                start(left_hop(slot))
+
+            @pl.when(low == chip)
+            def _():
+                add_total(strip, decode)
 
     piece = 16
     pieces = SLAB // piece
@@ -297,11 +372,13 @@
 
         @pl.when(j // slabs + 1 > chip)
         def _():
-            right_copy(j // slabs + 1, slab).wait_send()
+            for copy in right_hop(right_slot(j // slabs + 1, slab)):
+                copy.wait_send()
 
         @pl.when(j // slabs < chip)
         def _():
-            left_copy(j // slabs, slab).wait_send()
+            for copy in left_hop(left_slot(j // slabs, slab)):
+                copy.wait_send()
 
     for copy in square_copies + cross_copies:
         copy.wait_send()
@@ -376,8 +453,11 @@
         scratch_shapes=[
             pltpu.VMEM((chips, *tiled), jnp.bfloat16),
             pltpu.VMEM((chips, *tiled), jnp.bfloat16),
-            pltpu.VMEM((chips - 1, *tiled), F32),
-            pltpu.VMEM((chips - 1, *tiled), F32),
+            pltpu.VMEM((items, SLAB, cols), jnp.int16),
+            pltpu.VMEM((items, SLAB, cols), jnp.int16),
+            pltpu.VMEM((items, 1, cols), F32),
+            pltpu.VMEM((items, 1, cols), F32),
+            pltpu.VMEM((SLAB, cols), F32),
             pltpu.VMEM(tiled, F32),
             pltpu.VMEM(tiled, jnp.int32),
             pltpu.VMEM(tiled, jnp.int32),
@@ -392,10 +472,8 @@
             dma((chips * slabs,)),
             dma((chips * slabs,)),
             dma((chips * slabs,)),
-            dma((items,)),
-            dma((items,)),
-            dma((items,)),
-            dma((items,)),
+            dma((4, items)),
+            dma((4, items)),
             dma((2,)),
             dma((2, slabs)),
             dma((2, fsdp - 1)),

time: 311 us -> 179 us (0.58)
  Pallas kernels: 310 us -> 178 us
    pallas_call x1, Pallas kernels: 299 us -> 168 us  [local(): pl.pallas_call(functools.partial(exchange_kernel, chips, fsdp, sections,...]
where the time goes in v1:
time: 179 us
  Pallas kernels  178 us (99%)
    pallas_call x1, Pallas kernels, local(): pl.pallas_call(functools.partial(exchange_kernel, chips, fsdp, sections,...  168 us
    pallas_call x1, Pallas kernels, local(): pl.pallas_call(finish_kernel, grid=(slabs,), out_shape=(jax.ShapeDtypeStr...  10.4 us

profile of v1, /device:TPU:0, one launch (start us, length us, event | category | flops | bytes accessed | tf_op | source)
XLA Modules:
  0.0 179.0 jit_solution(14207533841566196634)
XLA Ops:
  0.6 167.9 %shard_map.126 = (f32[8,128,1024]{2,1,0:T(8,128)}, f32[8,128,1024]{2,1,0:T(8,128)}, f32[1,1024]{1,0:T(1,128)}, f32[1,1024]{1,0:T(1,128)}) custom-call(bf16[4,2,8,128,1024]{4,3,2,1,0:T(8,128)(2,1)} %bitcast.6, s32[8,128,1024]{2,1,0:T(8,128)} %bitcast.7, f32[1,1024]{1,0:T(1,128)} %first_rows.1, f32[1,1024]{1,0:T(1,128)} %first_cols.1, ...), custom_call_target="tpu_custom_call" | custom-call | tf_op jit(solution)/shard_map/pallas_call | solution.py:443
  168.5 10.4 %shard_map.127 = (f32[8,128,1024]{2,1,0:T(8,128)}, f32[8,128,1024]{2,1,0:T(8,128)}, f32[8,128,1024]{2,1,0:T(8,128)}, f32[1,1024]{1,0:T(1,128)}, f32[1,1024]{1,0:...) custom-call(f32[8,128,1024]{2,1,0:T(8,128)} %get-tuple-element.18.first, f32[8,128,1024]{2,1,0:T(8,128)} %get-tuple-element.19.second, ...), custom_call_target="tpu_custom_call" | custom-call | tf_op jit(solution)/shard_map/pallas_call | solution.py:498

commit v2 on v1

--- a/solution.py
+++ b/solution.py
@@ -21,7 +21,8 @@
 PIECE = 16
 LEVELS = 32767.0
 TINY = 1e-37
-VMEM_BYTES = 67043328
+EXCHANGE_VMEM = 44 * 2**20
+FINISH_VMEM = 10 * 2**20
 F32 = jnp.float32
 
 
@@ -38,8 +39,13 @@
     second_codes,
     second_rows,
     second_cols,
-    first_out,
-    second_out,
+    direction,
+    first,
+    second,
+    first_inverse,
+    second_inverse,
+    first_rowmax,
+    second_rowmax,
     first_colmax,
     second_colmax,
     own,
@@ -52,8 +58,8 @@
     total,
     codes_a,
     codes_b,
-    first,
-    second,
+    first_peak,
+    second_peak,
     square_send,
     square_recv,
     cross_send,
@@ -66,7 +72,6 @@
     right_sems,
     left_sems,
     code_sem,
-    out_sem,
     square_sems,
     cross_sems,
     col_sems,
@@ -330,37 +335,54 @@
     norm = jnp.sqrt(jnp.broadcast_to(square_sum, (1, cols)))
     scale = clip_limit / jnp.maximum(norm, clip_limit)
 
-    def out_copies(slab):
-        return (
-            pltpu.make_async_copy(first.at[slab], first_out.at[slab], out_sem.at[0, slab]),
-            pltpu.make_async_copy(second.at[slab], second_out.at[slab], out_sem.at[1, slab]),
-        )
-
-    def update_slab(slab, carry):
-        def update_piece(i, carry):
-            first_top, second_top = carry
-            rows = pl.ds(pl.multiple_of(i * piece, piece), piece)
-            clipped = scale * total[slab, rows, :]
-            first_new = first[slab, rows, :] + (1.0 - beta_first) * clipped
-            second_new = second[slab, rows, :] + (1.0 - beta_second) * clipped * clipped
-            first[slab, rows, :] = first_new
-            second[slab, rows, :] = second_new
-            high = jnp.max(jnp.abs(first_new).reshape(piece // 8, 8, cols), axis=0)
-            top = jnp.max(second_new.reshape(piece // 8, 8, cols), axis=0)
-            return jnp.maximum(first_top, high), jnp.maximum(second_top, top)
-
-        carry = lax.fori_loop(0, pieces, update_piece, carry)
-        for copy in out_copies(slab):
-            copy.start()
-        return carry
+    def update_piece(i, carry):
+        first_top, second_top = carry
+        slab, rows = i // pieces, piece_rows(i % pieces)
+        clipped = scale * total[slab, rows, :]
+        first_new = first[slab, rows, :] + (1.0 - beta_first) * clipped
+        second_new = second[slab, rows, :] + (1.0 - beta_second) * clipped * clipped
+        first[slab, rows, :] = first_new
+        second[slab, rows, :] = second_new
+        high = jnp.max(jnp.abs(first_new).reshape(piece // 8, 8, cols), axis=0)
+        top = jnp.max(second_new.reshape(piece // 8, 8, cols), axis=0)
+        return jnp.maximum(first_top, high), jnp.maximum(second_top, top)
 
     nothing = jnp.zeros((8, cols), F32)
-    first_top, second_top = lax.fori_loop(0, slabs, update_slab, (nothing, nothing))
+    first_top, second_top = lax.fori_loop(
+        0, slabs * pieces, update_piece, (nothing, nothing)
+    )
     first_top = jnp.max(first_top, axis=0, keepdims=True)
     second_top = jnp.max(second_top, axis=0, keepdims=True)
     col_send[0:1, :] = first_top
     col_send[1:2, :] = second_top
     col_copies = to_all("fsdp", fsdp, me, col_send, col_recv, col_sems)
+
+    def lane_peak(block):
+        peak = block[:, :LANES]
+        for q in range(1, cols // LANES):
+            peak = jnp.maximum(peak, block[:, q * LANES : (q + 1) * LANES])
+        return peak
+
+    @pl.loop(0, slabs)
+    def _(slab):
+        @pl.loop(0, pieces)
+        def _(i):
+            rows = piece_rows(i)
+            first_new = first[slab, rows, :]
+            second_new = second[slab, rows, :]
+            direction[slab, rows, :] = first_new / (jnp.sqrt(second_new) + epsilon)
+            first_peak[rows, :] = lane_peak(jnp.abs(first_new))
+            second_peak[rows, :] = lane_peak(second_new)
+
+        span = pl.ds(pl.multiple_of(slab * SLAB, SLAB), SLAB)
+        first_row = jnp.max(first_peak[...], axis=1, keepdims=True)
+        first_row = jnp.broadcast_to(jnp.maximum(first_row, scale_floor), (SLAB, LANES))
+        second_row = jnp.max(second_peak[...], axis=1, keepdims=True)
+        second_row = jnp.broadcast_to(second_row, (SLAB, LANES))
+        first_inverse[slab] = 1.0 / first_row
+        second_inverse[slab] = 1.0 / second_row
+        first_rowmax[:, span] = first_row.T[0:1, :]
+        second_rowmax[:, span] = second_row.T[0:1, :]
 
     @pl.loop(0, chips * slabs)
     def _(i):
@@ -392,36 +414,84 @@
     for copy in col_copies:
         copy.wait_send()
 
+
+def finish_kernel(
+    direction,
+    first,
+    second,
+    first_inverse,
+    second_inverse,
+    first_rowmax,
+    second_rowmax,
+    first_colmax,
+    second_colmax,
+    direction_out,
+    first_out,
+    second_out,
+    first_row_out,
+    first_col_out,
+    second_row_out,
+    second_col_out,
+    first_scaled,
+    second_scaled,
+    direction_sem,
+    out_sem,
+    small_sem,
+):
+    slabs, _, cols = first.shape
+    small = (
+        (first_rowmax, first_row_out),
+        (first_colmax, first_col_out),
+        (second_rowmax, second_row_out),
+        (second_colmax, second_col_out),
+    )
+    copies = [
+        pltpu.make_async_copy(direction.at[slab], direction_out.at[slab], direction_sem.at[slab])
+        for slab in range(slabs)
+    ]
+    copies += [
+        pltpu.make_async_copy(source, target, small_sem.at[i])
+        for i, (source, target) in enumerate(small)
+    ]
+    for copy in copies:
+        copy.start()
+    first_col = 1.0 / first_colmax[...]
+    second_col = 1.0 / second_colmax[...]
+
+    def out_copies(slab):
+        return (
+            pltpu.make_async_copy(first_scaled.at[slab], first_out.at[slab], out_sem.at[0, slab]),
+            pltpu.make_async_copy(
+                second_scaled.at[slab], second_out.at[slab], out_sem.at[1, slab]
+            ),
+        )
+
+    @pl.loop(0, slabs)
+    def _(slab):
+        @pl.loop(0, SLAB // PIECE)
+        def _(i):
+            rows = pl.ds(pl.multiple_of(i * PIECE, PIECE), PIECE)
+            first_row = first_inverse[slab, rows, :]
+            second_row = second_inverse[slab, rows, :]
+            for q in range(cols // LANES):
+                span = slice(q * LANES, (q + 1) * LANES)
+                first_scaled[slab, rows, span] = first[slab, rows, span] * jnp.maximum(
+                    first_row, first_col[:, span]
+                )
+                second_scaled[slab, rows, span] = second[slab, rows, span] * jnp.maximum(
+                    second_row, second_col[:, span]
+                )
+
+        for copy in out_copies(slab):
+            copy.start()
+
+    for copy in copies:
+        copy.wait()
+
     @pl.loop(0, slabs)
     def _(slab):
         for copy in out_copies(slab):
             copy.wait()
-
-
-def finish_kernel(
-    first,
-    second,
-    first_colmax,
-    second_colmax,
-    direction,
-    first_scaled,
-    second_scaled,
-    first_rowmax,
-    second_rowmax,
-    first_kept,
-    second_kept,
-):
-    first_new = first[0]
-    second_new = second[0]
-    first_top = jnp.maximum(jnp.max(jnp.abs(first_new), axis=1, keepdims=True), scale_floor)
-    second_top = jnp.max(second_new, axis=1, keepdims=True)
-    direction[0] = first_new / (jnp.sqrt(second_new) + epsilon)
-    first_scaled[0] = first_new / jnp.minimum(first_top, first_colmax[...])
-    second_scaled[0] = second_new / jnp.minimum(second_top, second_colmax[...])
-    first_rowmax[...] = jnp.broadcast_to(first_top, (SLAB, LANES)).T[0:1, :]
-    second_rowmax[...] = jnp.broadcast_to(second_top, (SLAB, LANES)).T[0:1, :]
-    first_kept[...] = first_colmax[...]
-    second_kept[...] = second_colmax[...]
 
 
 def local(
@@ -440,16 +510,13 @@
     hbm = pl.BlockSpec(memory_space=pl.ANY)
     vmem = pl.BlockSpec(memory_space=pltpu.VMEM)
     dma = pltpu.SemaphoreType.DMA
-    first_new, second_new, first_colmax, second_colmax = pl.pallas_call(
+    inverse = (slabs, SLAB, LANES)
+    kept = (tiled, tiled, tiled, inverse, inverse, (1, rows), (1, rows), (1, cols), (1, cols))
+    held = pl.pallas_call(
         functools.partial(exchange_kernel, chips, fsdp, sections, slabs, clip_limit),
-        out_shape=(
-            jax.ShapeDtypeStruct(tiled, F32),
-            jax.ShapeDtypeStruct(tiled, F32),
-            jax.ShapeDtypeStruct((1, cols), F32),
-            jax.ShapeDtypeStruct((1, cols), F32),
-        ),
+        out_shape=tuple(pltpu.VMEM(shape, F32) for shape in kept),
         in_specs=[hbm, hbm, vmem, vmem, hbm, vmem, vmem],
-        out_specs=(hbm, hbm, vmem, vmem),
+        out_specs=(vmem,) * len(kept),
         scratch_shapes=[
             pltpu.VMEM((chips, *tiled), jnp.bfloat16),
             pltpu.VMEM((chips, *tiled), jnp.bfloat16),
@@ -461,8 +528,8 @@
             pltpu.VMEM(tiled, F32),
             pltpu.VMEM(tiled, jnp.int32),
             pltpu.VMEM(tiled, jnp.int32),
-            pltpu.VMEM(tiled, F32),
-            pltpu.VMEM(tiled, F32),
+            pltpu.VMEM((SLAB, LANES), F32),
+            pltpu.VMEM((SLAB, LANES), F32),
             pltpu.VMEM((8, LANES), F32),
             pltpu.VMEM((fsdp - 1, 8, LANES), F32),
             pltpu.VMEM((8, LANES), F32),
@@ -475,13 +542,12 @@
             dma((4, items)),
             dma((4, items)),
             dma((2,)),
-            dma((2, slabs)),
             dma((2, fsdp - 1)),
             dma((2, max(sections - 1, 1))),
             dma((2, fsdp - 1)),
         ],
         compiler_params=pltpu.CompilerParams(
-            has_side_effects=True, vmem_limit_bytes=VMEM_BYTES
+            has_side_effects=True, vmem_limit_bytes=EXCHANGE_VMEM
         ),
     )(
         grads,
@@ -492,26 +558,30 @@
         second_rows,
         second_columns,
     )
-    block = pl.BlockSpec((1, SLAB, cols), lambda i: (i, 0, 0))
-    whole = pl.BlockSpec((1, cols), lambda i: (0, 0))
-    strip = pl.BlockSpec((1, SLAB), lambda i: (0, i))
     finished = pl.pallas_call(
         finish_kernel,
-        grid=(slabs,),
         out_shape=(
             jax.ShapeDtypeStruct(tiled, F32),
             jax.ShapeDtypeStruct(tiled, F32),
             jax.ShapeDtypeStruct(tiled, F32),
             jax.ShapeDtypeStruct((1, rows), F32),
+            jax.ShapeDtypeStruct((1, cols), F32),
             jax.ShapeDtypeStruct((1, rows), F32),
             jax.ShapeDtypeStruct((1, cols), F32),
-            jax.ShapeDtypeStruct((1, cols), F32),
         ),
-        in_specs=[block, block, whole, whole],
-        out_specs=(block, block, block, strip, strip, whole, whole),
-    )(first_new, second_new, first_colmax, second_colmax)
+        in_specs=[vmem] * len(kept),
+        out_specs=(hbm,) * 7,
+        scratch_shapes=[
+            pltpu.VMEM(tiled, F32),
+            pltpu.VMEM(tiled, F32),
+            dma((slabs,)),
+            dma((2, slabs)),
+            dma((4,)),
+        ],
+        compiler_params=pltpu.CompilerParams(vmem_limit_bytes=FINISH_VMEM),
+    )(*(pltpu.with_memory_space_constraint(x, pltpu.VMEM) for x in held))
     direction, first_scaled, second_scaled = finished[:3]
-    first_rowmax, second_rowmax, first_colmax, second_colmax = finished[3:]
+    first_rowmax, first_colmax, second_rowmax, second_colmax = finished[3:]
     shape = (layers, rows, cols)
     return (
         direction.reshape(shape),

time: 179 us -> 175 us (0.978)
  Pallas kernels: 178 us -> 174 us
    pallas_call x1, Pallas kernels: 10.4 us -> 4.8 us  [local(): pl.pallas_call(finish_kernel, out_shape=(jax.ShapeDtypeStruct(tiled, F32)...]
where the time goes in v2:
time: 175 us; the launch traced here: 174 us
  Pallas kernels  174 us (99%)
    pallas_call x1, Pallas kernels, local(): pl.pallas_call(functools.partial(exchange_kernel, chips, fsdp, sections,...  169 us
    pallas_call x1, Pallas kernels, local(): pl.pallas_call(finish_kernel, out_shape=(jax.ShapeDtypeStruct(tiled, F32)...  4.8 us

profile of v2, /device:TPU:0, one launch (start us, length us, event | category | flops | bytes accessed | tf_op | source)
XLA Modules:
  0.0 174.3 jit_solution(7345557731245377781)
XLA Ops:
  0.6 168.9 %shard_map.126 = (f32[8,128,1024]{2,1,0:T(8,128)S(1)}, f32[8,128,1024]{2,1,0:T(8,128)S(1)}, f32[8,128,1024]{2,1,0:T(8,128)S(1)}, f32[8,128,128]{2,1,0:T(8,128)S(...) custom-call(bf16[4,2,8,128,1024]{4,3,2,1,0:T(8,128)(2,1)} %bitcast.6, ...), custom_call_target="tpu_custom_call" | custom-call | tf_op jit(solution)/shard_map/pallas_call | solution.py:515
  169.5 4.8 %shard_map.127 = (f32[8,128,1024]{2,1,0:T(8,128)}, f32[8,128,1024]{2,1,0:T(8,128)}, f32[8,128,1024]{2,1,0:T(8,128)}, f32[1,1024]{1,0:T(1,128)}, f32[1,1024]{1,0:...) custom-call(f32[8,128,1024]{2,1,0:T(8,128)S(1)} %get-tuple-element.23.direction, ...), custom_call_target="tpu_custom_call" | custom-call | tf_op jit(solution)/shard_map/pallas_call | solution.py:561

commit v3 on v2

--- a/solution.py
+++ b/solution.py
@@ -19,6 +19,7 @@
 LANES = 128
 LAG = 2
 PIECE = 16
+UNROLL = 4
 LEVELS = 32767.0
 TINY = 1e-37
 EXCHANGE_VMEM = 44 * 2**20
@@ -62,8 +63,6 @@
     second_peak,
     square_send,
     square_recv,
-    cross_send,
-    cross_recv,
     col_send,
     col_recv,
     own_sem,
@@ -73,8 +72,8 @@
     left_sems,
     code_sem,
     square_sems,
-    cross_sems,
     col_sems,
+    ready,
 ):
     me = lax.axis_index("fsdp")
     section = lax.axis_index("section")
@@ -186,12 +185,41 @@
     def joined(decode, pair):
         return lambda rows: decode(rows) + pair(rows)
 
+    def in_order(i):
+        step, slab = i // slabs, i % slabs
+        return jnp.where(2 * chip < chips, chips - 1 - step, step), slab
+
+    def section_peer(s):
+        return {"section": (section + s) % sections}
+
+    def greet(semaphore, device):
+        pl.semaphore_signal(
+            semaphore, inc=1, device_id=device, device_id_type=pl.DeviceIdType.MESH
+        )
+
+    barrier = pltpu.get_barrier_semaphore()
+    greet(barrier, {"fsdp": partner})
+    for s in range(1, sections):
+        greet(barrier, section_peer(s))
+
+    @pl.when(chip > 0)
+    def _():
+        greet(barrier, {"fsdp": left})
+
+    @pl.when(chip < chips - 1)
+    def _():
+        greet(barrier, {"fsdp": right})
+
     @pl.loop(0, chips * slabs)
     def _(i):
-        step, slab = i // slabs, i % slabs
-        dest = jnp.where(2 * chip < chips, chips - 1 - step, step)
-        own_copy(dest, slab).start()
-        part_copy(dest, slab).start()
+        own_copy(*in_order(i)).start()
+
+    ends = (chip == 0).astype(jnp.int32) + (chip == chips - 1).astype(jnp.int32)
+    pl.semaphore_wait(barrier, sections + 2 - ends)
+
+    @pl.loop(0, chips * slabs)
+    def _(i):
+        part_copy(*in_order(i)).start()
 
     code_copies = (
         pltpu.make_async_copy(first_codes, codes_a, code_sem.at[0]),
@@ -252,6 +280,11 @@
 
     @pl.loop(0, items + LAG * (chips - 1))
     def _(step):
+        @pl.when(step == LAG * chips)
+        def _():
+            for s in range(1, sections):
+                greet(ready, section_peer(s))
+
         j = step - right_lag
         dest = chips - 1 - j // slabs
         slab = j % slabs
@@ -292,18 +325,22 @@
             def _():
                 add_total(strip, decode)
 
-    piece = 16
-    pieces = SLAB // piece
+    pieces = SLAB // PIECE
+
+    def fold(value):
+        return value.reshape(PIECE // 8, 8, cols)
 
     def add_squares(i, acc):
-        slab, rows = i // pieces, pl.ds(pl.multiple_of((i % pieces) * piece, piece), piece)
-        g = total[slab, rows, :]
-        return acc + jnp.sum((g * g).reshape(piece // 8, 8, cols), axis=0)
-
-    squares = lax.fori_loop(0, slabs * pieces, add_squares, jnp.zeros((8, cols), F32))
+        g = total[i // pieces, piece_rows(i % pieces), :]
+        return acc + jnp.sum(fold(g * g), axis=0)
+
+    squares = lax.fori_loop(
+        0, slabs * pieces, add_squares, jnp.zeros((8, cols), F32), unroll=UNROLL
+    )
     folded = squares[:, :LANES]
     for q in range(1, cols // LANES):
         folded = folded + squares[:, q * LANES : (q + 1) * LANES]
+    folded = jnp.sum(folded, axis=0, keepdims=True)
 
     def to_all(axis, size, position, source, slots, sems):
         copies = [
@@ -321,35 +358,54 @@
             copy.start()
         return copies
 
+    def square_copy(k):
+        return pltpu.make_async_remote_copy(
+            src_ref=square_send,
+            dst_ref=square_recv.at[k - 1],
+            send_sem=square_sems.at[0, k - 1],
+            recv_sem=square_sems.at[1, k - 1],
+            device_id={
+                "section": (section + k // fsdp) % sections,
+                "fsdp": (me + k % fsdp) % fsdp,
+            },
+            device_id_type=pl.DeviceIdType.MESH,
+        )
+
+    def add_square(k, acc):
+        square_copy(k).wait_recv()
+        return acc + square_recv[k - 1]
+
     square_send[...] = folded
-    square_copies = to_all("fsdp", fsdp, me, square_send, square_recv, square_sems)
-    for s, copy in enumerate(square_copies):
-        copy.wait_recv()
-        folded = folded + square_recv[s]
-    cross_send[...] = folded
-    cross_copies = to_all("section", sections, section, cross_send, cross_recv, cross_sems)
-    for s, copy in enumerate(cross_copies):
-        copy.wait_recv()
-        folded = folded + cross_recv[s]
-    square_sum = jnp.sum(jnp.sum(folded, axis=0, keepdims=True), axis=1, keepdims=True)
+    pl.semaphore_wait(ready, sections - 1)
+    devices = sections * fsdp
+
+    @pl.loop(1, devices)
+    def _(k):
+        square_copy(k).start()
+
+    folded = lax.fori_loop(1, devices, add_square, folded)
+    square_sum = jnp.sum(folded, axis=1, keepdims=True)
     norm = jnp.sqrt(jnp.broadcast_to(square_sum, (1, cols)))
     scale = clip_limit / jnp.maximum(norm, clip_limit)
-
-    def update_piece(i, carry):
+    first_gain = (1.0 - beta_first) * scale
+    second_gain = (1.0 - beta_second) * scale * scale
+
+    def moments(slab, rows):
+        g = total[slab, rows, :]
+        first_new = first[slab, rows, :] + first_gain * g
+        second_new = second[slab, rows, :] + second_gain * g * g
+        return first_new, second_new
+
+    def raise_tops(i, carry):
         first_top, second_top = carry
-        slab, rows = i // pieces, piece_rows(i % pieces)
-        clipped = scale * total[slab, rows, :]
-        first_new = first[slab, rows, :] + (1.0 - beta_first) * clipped
-        second_new = second[slab, rows, :] + (1.0 - beta_second) * clipped * clipped
-        first[slab, rows, :] = first_new
-        second[slab, rows, :] = second_new
-        high = jnp.max(jnp.abs(first_new).reshape(piece // 8, 8, cols), axis=0)
-        top = jnp.max(second_new.reshape(piece // 8, 8, cols), axis=0)
-        return jnp.maximum(first_top, high), jnp.maximum(second_top, top)
+        first_new, second_new = moments(i // pieces, piece_rows(i % pieces))
+        first_top = jnp.maximum(first_top, jnp.max(fold(jnp.abs(first_new)), axis=0))
+        second_top = jnp.maximum(second_top, jnp.max(fold(second_new), axis=0))
+        return first_top, second_top
 
     nothing = jnp.zeros((8, cols), F32)
     first_top, second_top = lax.fori_loop(
-        0, slabs * pieces, update_piece, (nothing, nothing)
+        0, slabs * pieces, raise_tops, (nothing, nothing), unroll=UNROLL
     )
     first_top = jnp.max(first_top, axis=0, keepdims=True)
     second_top = jnp.max(second_top, axis=0, keepdims=True)
@@ -365,11 +421,12 @@
 
     @pl.loop(0, slabs)
     def _(slab):
-        @pl.loop(0, pieces)
+        @pl.loop(0, pieces, unroll=UNROLL)
         def _(i):
             rows = piece_rows(i)
-            first_new = first[slab, rows, :]
-            second_new = second[slab, rows, :]
+            first_new, second_new = moments(slab, rows)
+            first[slab, rows, :] = first_new
+            second[slab, rows, :] = second_new
             direction[slab, rows, :] = first_new / (jnp.sqrt(second_new) + epsilon)
             first_peak[rows, :] = lane_peak(jnp.abs(first_new))
             second_peak[rows, :] = lane_peak(second_new)
@@ -402,8 +459,9 @@
             for copy in left_hop(left_slot(j // slabs, slab)):
                 copy.wait_send()
 
-    for copy in square_copies + cross_copies:
-        copy.wait_send()
+    @pl.loop(1, devices)
+    def _(k):
+        square_copy(k).wait_send()
 
     for s, copy in enumerate(col_copies):
         copy.wait_recv()
@@ -468,7 +526,7 @@
 
     @pl.loop(0, slabs)
     def _(slab):
-        @pl.loop(0, SLAB // PIECE)
+        @pl.loop(0, SLAB // PIECE, unroll=UNROLL)
         def _(i):
             rows = pl.ds(pl.multiple_of(i * PIECE, PIECE), PIECE)
             first_row = first_inverse[slab, rows, :]
@@ -530,10 +588,8 @@
             pltpu.VMEM(tiled, jnp.int32),
             pltpu.VMEM((SLAB, LANES), F32),
             pltpu.VMEM((SLAB, LANES), F32),
-            pltpu.VMEM((8, LANES), F32),
-            pltpu.VMEM((fsdp - 1, 8, LANES), F32),
-            pltpu.VMEM((8, LANES), F32),
-            pltpu.VMEM((max(sections - 1, 1), 8, LANES), F32),
+            pltpu.VMEM((1, LANES), F32),
+            pltpu.VMEM((sections * fsdp - 1, 1, LANES), F32),
             pltpu.VMEM((2, cols), F32),
             pltpu.VMEM((fsdp - 1, 2, cols), F32),
             dma((chips * slabs,)),
@@ -542,12 +598,12 @@
             dma((4, items)),
             dma((4, items)),
             dma((2,)),
+            dma((2, sections * fsdp - 1)),
             dma((2, fsdp - 1)),
-            dma((2, max(sections - 1, 1))),
-            dma((2, fsdp - 1)),
+            pltpu.SemaphoreType.REGULAR,
         ],
         compiler_params=pltpu.CompilerParams(
-            has_side_effects=True, vmem_limit_bytes=EXCHANGE_VMEM
+            has_side_effects=True, collective_id=0, vmem_limit_bytes=EXCHANGE_VMEM
         ),
     )(
         grads,

time: 175 us -> 167 us (0.954)
  Pallas kernels: 174 us -> 166 us
    pallas_call x1, Pallas kernels: 169 us -> 161 us  [local(): pl.pallas_call(functools.partial(exchange_kernel, chips, fsdp, sections,...]
where the time goes in v3:
time: 167 us; the launch traced here: 166 us
  Pallas kernels  166 us (99%)
    pallas_call x1, Pallas kernels, local(): pl.pallas_call(functools.partial(exchange_kernel, chips, fsdp, sections,...  161 us
    pallas_call x1, Pallas kernels, local(): pl.pallas_call(finish_kernel, out_shape=(jax.ShapeDtypeStruct(tiled, F32)...  4.8 us

profile of v3, /device:TPU:0, one launch (start us, length us, event | category | flops | bytes accessed | tf_op | source)
XLA Modules:
  0.0 166.4 jit_solution(14181516040648719266)
XLA Ops:
  0.6 161.0 %shard_map.126 = (f32[8,128,1024]{2,1,0:T(8,128)S(1)}, f32[8,128,1024]{2,1,0:T(8,128)S(1)}, f32[8,128,1024]{2,1,0:T(8,128)S(1)}, f32[8,128,128]{2,1,0:T(8,128)S(...) custom-call(bf16[4,2,8,128,1024]{4,3,2,1,0:T(8,128)(2,1)} %bitcast.6, ...), custom_call_target="tpu_custom_call" | custom-call | tf_op jit(solution)/shard_map/pallas_call | solution.py:573
  161.6 4.8 %shard_map.127 = (f32[8,128,1024]{2,1,0:T(8,128)}, f32[8,128,1024]{2,1,0:T(8,128)}, f32[8,128,1024]{2,1,0:T(8,128)}, f32[1,1024]{1,0:T(1,128)}, f32[1,1024]{1,0:...) custom-call(f32[8,128,1024]{2,1,0:T(8,128)S(1)} %get-tuple-element.23.direction, ...), custom_call_target="tpu_custom_call" | custom-call | tf_op jit(solution)/shard_map/pallas_call | solution.py:617
